TPU v7x, 32 devices: a whole 2x2x4 slice. The times are simulated.
32 devices in a mesh: grp: 2 (over x), sub: 16 (over z, y, core).
Axes of the slice: x: 2, y: 2, z: 4, core: 2. Of those that a mesh axis runs over, the one named last changes fastest.
Arguments:
- counts: int32 [32], P(('grp', 'sub')), may hold values from 1 to 3, as said below
- block_map: int32 [96], P(('grp', 'sub')), may hold values from 0 to 31
- perms: int32 [96, 256], P(('grp', 'sub')), may hold values from 0 to 255, each once within a row
- mass_ii: bfloat16 [96, 1024, 1024], P(('grp', 'sub')), may hold values from -0.005859375 to 0.005859375
- mass_ib: bfloat16 [96, 1024, 256], P(('grp', 'sub')), may hold values from -0.1875 to 0.1875
- mass_bb: bfloat16 [96, 256, 256], P(('grp', 'sub')), may hold values from -6 to 6
- constraint_modes: bfloat16 [96, 1024, 256], P(('grp', 'sub')), may hold values from -6 to 6
- fixed_modes: bfloat16 [96, 1024, 128], P(('grp', 'sub')), may hold values from -6 to 6
Outputs:
- blocks: float32 [32, 256, 256], P('grp', 'sub')
- coupling: float32 [96, 128, 256], P(('grp', 'sub'))
Inputs may be any that keep to these rules, and one draw needn't show every extreme that they name: `counts`: at least one device uses all 3 slots and one uses a single slot.
All inputs are finite; a program needn't handle non-finite values.
Results may differ from a plain program's by a relative error of at most 0.0021.
Values sent between devices are 32-bit elements; how exact they have to be, the bound alone decides.
No kernel may reach another device: no remote copies, remote signals or barrier semaphores. Data moves between devices by JAX's collectives and lax.ppermute only.
A program may use at most 128 MiB of HBM per device.

v0:
```python
import jax
import jax.numpy as jnp
from jax import lax
from jax.sharding import PartitionSpec as P

NBG = 16


def shifted(value, axis, by):
    peers = lax.axis_size(axis)
    return lax.ppermute(value, axis, [(i, (i + by) % peers) for i in range(peers)])


def contract(left, right):
    return lax.dot_general(
        left, right, (((0,), (0,)), ((), ())), preferred_element_type=jnp.float32
    )


def reduce_slot(mass_ii, mass_ib, mass_bb, constraint_modes, fixed_modes):
    product = jnp.dot(mass_ii, constraint_modes, preferred_element_type=jnp.float32).astype(
        jnp.bfloat16
    )
    cross = contract(constraint_modes, mass_ib)
    reduced = contract(constraint_modes, product) + cross + cross.T + mass_bb.astype(jnp.float32)
    coupled = contract(fixed_modes, product) + contract(fixed_modes, mass_ib)
    return (reduced, coupled)


def per_device(counts, block_map, perms, mass_ii, mass_ib, mass_bb, constraint_modes, fixed_modes):
    width = mass_bb.shape[1]
    modes = fixed_modes.shape[2]
    slot_total = mass_ii.shape[0]
    used_count = counts[0]
    sub_size = lax.axis_size("sub")

    def pick(array, slot_index):
        return lax.dynamic_index_in_dim(array, slot_index, 0, keepdims=False)

    start_parts = jnp.zeros((slot_total, width, width), jnp.float32)
    carry_state = (start_parts, jnp.zeros((slot_total, modes, width), jnp.float32))
    for slot_index in range(slot_total):
        one_parts, one_coupling = carry_state
        reduced, coupled = reduce_slot(
            pick(mass_ii, slot_index),
            pick(mass_ib, slot_index),
            pick(mass_bb, slot_index),
            pick(constraint_modes, slot_index),
            pick(fixed_modes, slot_index),
        )
        active = (slot_index < used_count).astype(jnp.float32)
        perm_row = pick(perms, slot_index)
        inverse = (
            jnp.zeros((width,), jnp.int32).at[perm_row].set(jnp.arange(width, dtype=jnp.int32))
        )
        placed = reduced[inverse][:, inverse] * active
        one_parts = lax.dynamic_update_index_in_dim(one_parts, placed, slot_index, 0)
        one_coupling = lax.dynamic_update_index_in_dim(
            one_coupling, coupled * active, slot_index, 0
        )
        carry_state = (one_parts, one_coupling)
    parts, coupling = carry_state
    slot_ids = jnp.arange(slot_total, dtype=jnp.int32)
    active_col = (slot_ids < used_count).astype(jnp.float32)
    targets = jnp.arange(2 * NBG, dtype=jnp.int32)
    one_hot = (block_map[:, None] == targets[None, :]).astype(jnp.float32) * active_col[:, None]
    spread_hot = jnp.broadcast_to(one_hot[:, None, :], (slot_total, sub_size, 2 * NBG))
    rows_in, hot_in = (
        lax.all_to_all(parts, "sub", split_axis=1, concat_axis=0, tiled=True),
        lax.all_to_all(spread_hot, "sub", split_axis=1, concat_axis=0, tiled=True),
    )
    hot_flat = hot_in[:, 0, :]
    owned = jnp.einsum("rc,rab->cab", hot_flat, rows_in, precision=lax.Precision.HIGHEST)
    home_rows = owned[:NBG]
    ahead_rows = owned[NBG:]
    blocks = home_rows + shifted(ahead_rows, "grp", 1)
    return (blocks, coupling)


def solution(mesh):
    placed = (
        P(("grp", "sub")),
        P(("grp", "sub")),
        P(("grp", "sub"), None),
        P(("grp", "sub"), None, None),
        P(("grp", "sub"), None, None),
        P(("grp", "sub"), None, None),
        P(("grp", "sub"), None, None),
        P(("grp", "sub"), None, None),
    )
    return jax.shard_map(
        per_device,
        mesh=mesh,
        in_specs=placed,
        out_specs=(P("grp", "sub", None), P(("grp", "sub"), None, None)),
        check_vma=False,
    )
```

profile of v0, /device:TPU:11, one launch (start us, length us, event | category | flops | bytes accessed | tf_op | source)
XLA Modules:
  0.0 96.7 jit_solution(16782596118019003462)
XLA Ops:
  0.6 0.0 copy-start
  1.4 0.7 fusion.83
  2.1 0.6 broadcast_in_dim.40
  2.8 6.6 %all-to-all-start = ((f32[3,16,32]{2,0,1:T(4,128)}), f32[3,16,32]{2,0,1:T(4,128)}, u32[]{:S(2)}, u32[]{:S(2)}) async-start(f32[3,16,32]{2,0,1:T(4,128)} %broadcast_in_dim.40), calls=%async_computation | async-start | bytes 65536 | tf_op jit(solution)/shard_map/all_to_all | solution.py:70
  9.3 2.2 %fusion.50 = f32[256,256]{1,0:T(8,128)} fusion(bf16[3,1024,256]{2,1,0:T(8,128)(2,1)} %param.12, bf16[3,1024,256]{2,1,0:T(8,128)(2,1)} %param.14), kind=kOutput, calls=%fused_computation.62 | convolution fusion | flops 134217728 | bytes 1310720 | tf_op jit(solution)/shard_map/dot_general | solution.py:15
  11.6 0.0 copy-done
  11.6 2.1 %fusion.38 = f32[256,256]{1,0:T(8,128)} fusion(bf16[3,1024,256]{2,1,0:T(8,128)(2,1)} %param.12, bf16[3,1024,256]{2,1,0:T(8,128)(2,1)S(1)} %copy-done), kind=kOutput, calls=%fused_computation.50 | convolution fusion | flops 134217728 | bytes 1310720 | tf_op jit(solution)/shard_map/dot_general | solution.py:15
  13.7 1.5 %fusion.44 = f32[256,256]{1,0:T(8,128)S(1)} fusion(bf16[3,1024,256]{2,1,0:T(8,128)(2,1)} %param.12, bf16[3,1024,256]{2,1,0:T(8,128)(2,1)S(1)} %copy-done), kind=kOutput, calls=%fused_computation.56 | convolution fusion | flops 134217728 | bytes 1310720 | tf_op jit(solution)/shard_map/dot_general | solution.py:15
  15.2 0.0 copy-start.3
  15.2 2.8 %fusion.9 = bf16[1024,256]{1,0:T(8,128)(2,1)S(1)} fusion(bf16[3,1024,1024]{2,1,0:T(8,128)(2,1)} %param.11, bf16[3,1024,256]{2,1,0:T(8,128)(2,1)S(1)} %copy-done), kind=kOutput, calls=%fused_computation.18 | convolution fusion | flops 537133056 | bytes 3145728 | tf_op jit(solution)/shard_map/dot_general | solution.py:21
  18.0 0.0 copy-done.10
  18.0 0.7 fusion.15
  18.7 0.0 copy-start.9
  18.7 0.7 fusion.12
  19.5 1.4 %scatter_custom_fusion = s32[256]{0:T(256)S(1)} fusion(s32[256]{0:T(256)S(1)} %bitcast.172, s32[256]{0:T(256)S(1)} %iota.22, s32[]{:T(128)} %constant.74.clone.1), kind=kCustom, calls=%fused_computation.115 | custom fusion | bytes 1028 | tf_op jit(solution)/shard_map/scatter | solution.py:54
  20.9 1.4 %scatter_custom_fusion.1 = s32[256]{0:T(256)S(1)} fusion(s32[256]{0:T(256)S(1)} %bitcast.171, s32[256]{0:T(256)S(1)} %iota.23, s32[]{:T(128)} %constant.74.clone.1), kind=kCustom, calls=%fused_computation.113 | custom fusion | bytes 1028 | tf_op jit(solution)/shard_map/scatter | solution.py:54
  22.3 1.4 %scatter_custom_fusion.2 = s32[256]{0:T(256)S(1)} fusion(s32[256]{0:T(256)S(1)} %bitcast.170, s32[256]{0:T(256)S(1)} %iota.24, s32[]{:T(128)} %constant.74.clone.1), kind=kCustom, calls=%fused_computation.111 | custom fusion | bytes 1028 | tf_op jit(solution)/shard_map/scatter | solution.py:54
  23.8 0.0 copy-done.3
  23.8 0.8 copy.53
  24.6 1.8 %copy.57 = f32[256,256]{0,1:T(8,128)} copy(f32[256,256]{1,0:T(8,128)} %fusion.38) | data formatting | bytes 524288 | tf_op jit(solution)/shard_map/dot_general | solution.py:15
  26.5 1.8 %copy.49 = f32[256,256]{0,1:T(8,128)} copy(f32[256,256]{1,0:T(8,128)} %fusion.50) | data formatting | bytes 524288 | tf_op jit(solution)/shard_map/dot_general | solution.py:15
  28.3 1.7 %fusion.90 = (bf16[1,256,256]{2,1,0:T(8,128)(2,1)}, bf16[1,256,256]{2,1,0:T(8,128)(2,1)}, bf16[1,256,256]{2,1,0:T(8,128)(2,1)S(1)}) fusion(bf16[3,256,256]{2,1,0:T(8,128)(2,1)} %param.13), kind=kLoop, calls=%fused_computation.117 | loop fusion | bytes 786432 | tf_op jit(solution)/shard_map/jit(dynamic_index_in_dim)/dynamic_slice | solution.py:38
  30.0 1.7 %copy.78 = bf16[1,256,256]{1,2,0:T(8,128)(2,1)} copy(bf16[1,256,256]{2,1,0:T(8,128)(2,1)} %get-tuple-element.8) | data formatting | bytes 262144
  31.7 1.7 %copy.77 = bf16[1,256,256]{1,2,0:T(8,128)(2,1)} copy(bf16[1,256,256]{2,1,0:T(8,128)(2,1)} %get-tuple-element.9) | data formatting | bytes 262144
  33.3 0.7 copy.76
  34.1 2.0 %fusion.26 = f32[256,256]{0,1:T(8,128)} fusion(f32[256,256]{0,1:T(8,128)} %copy.49, bf16[1024,256]{1,0:T(8,128)(2,1)S(1)} %fusion.9, bf16[3,1024,256]{2,1,0:T(8,128)(2,1)S(1)} %copy-done, f32[256,256]{1,0:T(8,128)S(1)} %copy-done.4, bf16[1,256,256]{1,2,0:T(8,128)(2,1)} %copy.76), kind=kOutput, calls=%fused_computation.32 | convolution fusion | flops 134479872 | bytes 1966080 | tf_op jit(solution)/shard_map/dot_general | solution.py:15
  36.1 1.1 %copy.51 = f32[256,256]{1,0:T(8,128)S(1)} copy(f32[256,256]{0,1:T(8,128)} %fusion.26) | data formatting | bytes 524288 | tf_op jit(solution)/shard_map/add | solution.py:25
  37.2 1.7 %gather_fusion = f32[256,256]{1,0:T(8,128)} fusion(f32[256,256]{1,0:T(8,128)S(1)} %copy.51, s32[1024]{0:T(1024)S(1)} %pad_clamp_fusion.2), kind=kCustom, calls=%fused_computation | custom fusion | bytes 525312 | tf_op jit(solution)/shard_map/gather | solution.py:56
  38.8 1.1 %copy.52 = f32[256,256]{0,1:T(8,128)S(1)} copy(f32[256,256]{1,0:T(8,128)} %gather_fusion) | data formatting | bytes 524288 | tf_op jit(solution)/shard_map/gather | solution.py:56
  40.0 1.7 %gather_fusion.1 = f32[256,256]{1,0:T(8,128)} fusion(f32[256,256]{0,1:T(8,128)S(1)} %copy.52, s32[1024]{0:T(1024)S(1)} %pad_clamp_fusion.2), kind=kCustom, calls=%fused_computation.1 | custom fusion | bytes 525312 | tf_op jit(solution)/shard_map/gather | solution.py:56
  41.6 2.1 %fusion.22 = f32[256,256]{0,1:T(8,128)} fusion(f32[256,256]{0,1:T(8,128)} %copy.57, bf16[1024,256]{1,0:T(8,128)(2,1)S(1)} %fusion.15, bf16[3,1024,256]{2,1,0:T(8,128)(2,1)S(1)} %copy-done, f32[256,256]{1,0:T(8,128)} %fusion.38, bf16[1,256,256]{1,2,0:T(8,128)(2,1)S(1)} %copy-done.8), kind=kOutput, calls=%fused_computation.28 | convolution fusion | flops 134479872 | bytes 1966080 | tf_op jit(solution)/shard_map/dot_general | solution.py:15
  43.7 1.1 %copy.59 = f32[256,256]{1,0:T(8,128)S(1)} copy(f32[256,256]{0,1:T(8,128)} %fusion.22) | data formatting | bytes 524288 | tf_op jit(solution)/shard_map/add | solution.py:25
  44.8 1.7 %gather_fusion.4 = f32[256,256]{1,0:T(8,128)} fusion(f32[256,256]{1,0:T(8,128)S(1)} %copy.59, s32[1024]{0:T(1024)S(1)} %pad_clamp_fusion), kind=kCustom, calls=%fused_computation.4 | custom fusion | bytes 525312 | tf_op jit(solution)/shard_map/gather | solution.py:56
  46.5 1.1 %copy.60 = f32[256,256]{0,1:T(8,128)S(1)} copy(f32[256,256]{1,0:T(8,128)} %gather_fusion.4) | data formatting | bytes 524288 | tf_op jit(solution)/shard_map/gather | solution.py:56
  47.6 1.7 %gather_fusion.5 = f32[256,256]{1,0:T(8,128)} fusion(f32[256,256]{0,1:T(8,128)S(1)} %copy.60, s32[1024]{0:T(1024)S(1)} %pad_clamp_fusion), kind=kCustom, calls=%fused_computation.5 | custom fusion | bytes 525312 | tf_op jit(solution)/shard_map/gather | solution.py:56
  49.2 1.4 %fusion.24 = f32[256,256]{0,1:T(8,128)S(1)} fusion(f32[256,256]{0,1:T(8,128)} %copy.53, bf16[1024,256]{1,0:T(8,128)(2,1)S(1)} %fusion.12, bf16[3,1024,256]{2,1,0:T(8,128)(2,1)S(1)} %copy-done, f32[256,256]{1,0:T(8,128)} %copy-done.3, bf16[1,256,256]{1,2,0:T(8,128)(2,1)S(1)} %copy-done.7), kind=kOutput, calls=%fused_computation.30 | convolution fusion | flops 134479872 | bytes 1966080 | tf_op jit(solution)/shard_map/dot_general | solution.py:15
  50.6 0.1 copy.55
  50.8 1.0 %gather_fusion.2 = f32[256,256]{1,0:T(8,128)S(1)} fusion(f32[256,256]{1,0:T(8,128)S(1)} %copy.55, s32[1024]{0:T(1024)S(1)} %pad_clamp_fusion.1), kind=kCustom, calls=%fused_computation.2 | custom fusion | bytes 525312 | tf_op jit(solution)/shard_map/gather | solution.py:56
  51.7 0.0 copy-start.1
  51.7 0.1 copy.56
  51.9 1.0 %gather_fusion.3 = f32[256,256]{1,0:T(8,128)S(1)} fusion(f32[256,256]{0,1:T(8,128)S(1)} %copy.56, s32[1024]{0:T(1024)S(1)} %pad_clamp_fusion.1), kind=kCustom, calls=%fused_computation.3 | custom fusion | bytes 525312 | tf_op jit(solution)/shard_map/gather | solution.py:56
  52.8 0.0 copy-done.1
  52.9 0.0 copy-start.2
  52.9 0.1 dynamic_update_slice.20
  53.0 0.8 copy-done.2
  53.8 1.3 %copy.61 = f32[3,256,256]{2,0,1:T(4,128)} copy(f32[3,256,256]{1,2,0:T(8,128)S(1)} %bitcast_dynamic-update-slice_fusion) | data formatting | bytes 1572864 | tf_op jit(solution)/shard_map/jit(dynamic_update_index_in_dim)/dynamic_update_slice | solution.py:57
  55.1 0.0 all-to-all-done
  55.1 6.0 %all-to-all-start.1 = ((f32[3,256,256]{2,0,1:T(4,128)}), f32[3,256,256]{2,0,1:T(4,128)S(1)}, u32[]{:S(2)}, u32[]{:S(2)}) async-start(f32[3,256,256]{2,0,1:T(4,128)} %copy.61), calls=%async_computation.1 | async-start | bytes 2097152 | tf_op jit(solution)/shard_map/all_to_all | solution.py:69
  61.2 1.4 %convolution_bitcast_fusion.5 = f32[128,256]{0,1:T(8,128)S(1)} fusion(bf16[1024,256]{1,0:T(8,128)(2,1)S(1)} %fusion.9, bf16[3,1024,128]{2,1,0:T(8,128)(2,1)} %param.15), kind=kOutput, calls=%fused_computation.46 | convolution fusion | flops 67108864 | bytes 917504 | tf_op jit(solution)/shard_map/dot_general | solution.py:15
  62.5 1.5 %fusion.34 = f32[1,128,256]{1,2,0:T(8,128)S(1)} fusion(f32[128,256]{0,1:T(8,128)S(1)} %convolution_bitcast_fusion.5, bf16[3,1024,256]{2,1,0:T(8,128)(2,1)} %param.12, bf16[3,1024,128]{2,1,0:T(8,128)(2,1)} %param.15, f32[]{:T(128)S(6)} %convert_element_type.48), kind=kOutput, calls=%fused_computation.45 | convolution fusion | flops 67174400 | bytes 1048580 | tf_op jit(solution)/shard_map/dot_general | solution.py:15
  64.0 0.3 convolution_bitcast_fusion.4
  64.4 1.4 %fusion.32 = f32[3,128,256]{1,2,0:T(8,128)S(1)} fusion(f32[3,128,256]{1,2,0:T(8,128)S(1)} %dynamic_update_slice.23, f32[128,256]{0,1:T(8,128)S(1)} %convolution_bitcast_fusion.4, bf16[3,1024,256]{2,1,0:T(8,128)(2,1)} %param.12, bf16[3,1024,128]{2,1,0:T(8,128)(2,1)S(1)} %copy-done.5, f32[]{:T(128)S(6)} %convert_element_type.52), kind=kOutput, calls=%fused_computation.41 | convolution fusion | flops 67174400 | bytes 1048580 | tf_op jit(solution)/shard_map/dot_general | solution.py:15
  65.8 0.8 squeeze.60
  66.6 19.5 %all-to-all-done.1 = f32[3,256,256]{2,0,1:T(4,128)S(1)} async-done(((f32[3,256,256]{2,0,1:T(4,128)}), f32[3,256,256]{2,0,1:T(4,128)S(1)}, u32[]{:S(2)}, u32[]{:S(2)}) %all-to-all-start.1) | async-done | bytes 786464 | tf_op jit(solution)/shard_map/all_to_all | solution.py:69
  86.1 0.2 copy.62
  86.2 0.0 copy-start.6
  86.3 0.1 copy.63
  86.3 1.0 %fusion.35 = f32[32,16,256]{2,0,1:T(8,128)S(1)} fusion(f32[48,16,256]{2,1,0:T(8,128)S(1)} %bitcast.169, f32[48,32]{1,0:T(8,128)S(1)} %squeeze.60), kind=kOutput, calls=%fused_computation.47 | convolution fusion | flops 75497472 | bytes 1316864 | tf_op jit(solution)/shard_map/rc,rab->cab/dot_general | solution.py:73
  87.4 0.3 collective-permute-start
  87.7 0.3 convolution_bitcast_fusion.3
  88.0 1.4 %fusion.29 = f32[3,128,256]{1,2,0:T(8,128)S(1)} fusion(f32[3,128,256]{1,2,0:T(8,128)S(1)} %fusion.32, f32[128,256]{0,1:T(8,128)S(1)} %convolution_bitcast_fusion.3, bf16[3,1024,256]{2,1,0:T(8,128)(2,1)} %param.12, bf16[3,1024,128]{2,1,0:T(8,128)(2,1)S(1)} %copy-done.6, f32[]{:T(128)S(6)} %convert_element_type.56), kind=kOutput, calls=%fused_computation.36 | convolution fusion | flops 67174400 | bytes 1048580 | tf_op jit(solution)/shard_map/dot_general | solution.py:15
  89.4 0.9 copy.70
  90.4 5.4 %collective-permute-done = f32[16,16,256]{2,0,1:T(8,128)S(1)} collective-permute-done((f32[16,16,256]{2,0,1:T(8,128)S(1)}, f32[16,16,256]{2,0,1:T(8,128)S(1)}, u32[]{:S(2)}, u32[]{:S(2)}) %collective-permute-start) | collective-permute-done | bytes 262176 | tf_op jit(solution)/shard_map/ppermute | solution.py:11
  95.8 0.9 copy.69
  (27 shorter events, 0.2 us)
Async XLA Ops:
  0.6 10.9 %copy-start = (bf16[3,1024,256]{2,1,0:T(8,128)(2,1)S(1)}, bf16[3,1024,256]{2,1,0:T(8,128)(2,1)}, u32[]{:S(2)}) copy-start(bf16[3,1024,256]{2,1,0:T(8,128)(2,1)} %param.14) | copy-start | bytes 4718596
  2.8 52.4 %all-to-all-start = ((f32[3,16,32]{2,0,1:T(4,128)}), f32[3,16,32]{2,0,1:T(4,128)}, u32[]{:S(2)}, u32[]{:S(2)}) async-start(f32[3,16,32]{2,0,1:T(4,128)} %broadcast_in_dim.40), calls=%async_computation | async-start | bytes 65536 | tf_op jit(solution)/shard_map/all_to_all | solution.py:70
  13.7 4.3 %copy-start.10 = (bf16[3,1024,1024]{2,1,0:T(8,128)(2,1)S(1)}, bf16[3,1024,1024]{2,1,0:T(8,128)(2,1)}, u32[]{:S(2)}) copy-start(bf16[3,1024,1024]{2,1,0:T(8,128)(2,1)} %param.11) | copy-start | bytes 18874372
  15.2 8.6 %copy-start.3 = (f32[256,256]{1,0:T(8,128)}, f32[256,256]{1,0:T(8,128)S(1)}, u32[]{:S(2)}) copy-start(f32[256,256]{1,0:T(8,128)S(1)} %fusion.44) | copy-start | bytes 786436
  18.7 0.7 copy-start.9
  24.6 9.4 %copy-start.4 = (f32[256,256]{1,0:T(8,128)S(1)}, f32[256,256]{1,0:T(8,128)}, u32[]{:S(2)}) copy-start(f32[256,256]{1,0:T(8,128)} %fusion.50) | copy-start | bytes 786436
  38.8 2.8 %copy-start.8 = (bf16[1,256,256]{1,2,0:T(8,128)(2,1)S(1)}, bf16[1,256,256]{1,2,0:T(8,128)(2,1)}, u32[]{:S(2)}) copy-start(bf16[1,256,256]{1,2,0:T(8,128)(2,1)} %copy.78) | copy-start | bytes 393220
  46.5 2.8 %copy-start.7 = (bf16[1,256,256]{1,2,0:T(8,128)(2,1)S(1)}, bf16[1,256,256]{1,2,0:T(8,128)(2,1)}, u32[]{:S(2)}) copy-start(bf16[1,256,256]{1,2,0:T(8,128)(2,1)} %copy.77) | copy-start | bytes 393220
  51.7 1.1 %copy-start.1 = (f32[256,256]{1,0:T(8,128)S(1)}, f32[256,256]{1,0:T(8,128)}, u32[]{:S(2)}) copy-start(f32[256,256]{1,0:T(8,128)} %gather_fusion.1) | copy-start | bytes 786436
  52.9 1.0 copy-start.2
  55.1 30.9 %all-to-all-start.1 = ((f32[3,256,256]{2,0,1:T(4,128)}), f32[3,256,256]{2,0,1:T(4,128)S(1)}, u32[]{:S(2)}, u32[]{:S(2)}) async-start(f32[3,256,256]{2,0,1:T(4,128)} %copy.61), calls=%async_computation.1 | async-start | bytes 2097152 | tf_op jit(solution)/shard_map/all_to_all | solution.py:69
  61.2 2.9 %copy-start.5 = (bf16[3,1024,128]{2,1,0:T(8,128)(2,1)S(1)}, bf16[3,1024,128]{2,1,0:T(8,128)(2,1)}, u32[]{:S(2)}) copy-start(bf16[3,1024,128]{2,1,0:T(8,128)(2,1)} %param.15) | copy-start | bytes 2359300
  86.2 1.5 %copy-start.6 = (bf16[3,1024,128]{2,1,0:T(8,128)(2,1)S(1)}, bf16[3,1024,128]{2,1,0:T(8,128)(2,1)}, u32[]{:S(2)}) copy-start(bf16[3,1024,128]{2,1,0:T(8,128)(2,1)} %param.15) | copy-start | bytes 2359300
  87.4 8.4 %collective-permute-start = (f32[16,16,256]{2,0,1:T(8,128)S(1)}, f32[16,16,256]{2,0,1:T(8,128)S(1)}, u32[]{:S(2)}, u32[]{:S(2)}) collective-permute-start(f32[16,16,256]{2,0,1:T(8,128)S(1)} %slice.39), channel_id=1, source_target_pairs={{0,16},{16,0},{1,17},{17,1},{2,18},{18,2},{3,19},{19,3},{4,20},{20... | collective-permute-start | bytes 786440 | tf_op jit(solution)/shard_map/ppermute | solution.py:11
where the time goes:
time: 97.5 us; the launch traced here: 96.7 us
  local copies, waits for them, and re-layouts  33.3 us (34%)
  waiting for transfers between devices  24.9 us (26%)
  matrix products  22.8 us (23%)
  starting transfers between devices  12.9 us (13%)
  between operations  1.81 us (2%)
    all_to_all x1, waiting for transfers between devices, per_device(): lax.all_to_all(parts, 'sub', split_axis=1, concat_axis=0, tiled=True)  19.5 us
    dot_general x12, matrix products, contract(): lax.dot_general(left, right, (((0,), (0,)), ((), ())), preferred_element_...  17.6 us
    gather x9, local copies, waits for them, and re-layouts, per_device(): placed = reduced[inverse][:, inverse] * active  11 us
    unnamed x27, local copies, waits for them, and re-layouts  6.7 us
    all_to_all x1, starting transfers between devices, per_device(): lax.all_to_all(spread_hot, 'sub', split_axis=1, concat_axis=0, tiled=True)  6.58 us
    all_to_all x1, starting transfers between devices, per_device(): lax.all_to_all(parts, 'sub', split_axis=1, concat_axis=0, tiled=True)  6.01 us
    ppermute x1, waiting for transfers between devices, shifted(): lax.ppermute(value, axis, [(i, (i + by) % peers) for i in range(peers)])  5.41 us
    dot_general x3, local copies, waits for them, and re-layouts, contract(): lax.dot_general(left, right, (((0,), (0,)), ((), ())), preferred_element_...  4.45 us
  transfers between devices with their start and end apart: 3, of which 2 were waited for; matrix products, arithmetic and copies ran while one was open for 54% of the time, Pallas kernels for 0%

commit v1 on v0

--- a/solution.py
+++ b/solution.py
@@ -28,6 +28,15 @@
 
 
 def per_device(counts, block_map, perms, mass_ii, mass_ib, mass_bb, constraint_modes, fixed_modes):
+
+    def attach_column_on_mesh(xx, link_axis, row_dim, array_dim):
+        return jnp.concatenate(
+            lax.all_to_all(
+                jnp.stack(jnp.split(xx, lax.axis_size(link_axis), axis=row_dim)), link_axis, 0, 0
+            ),
+            axis=array_dim,
+        )
+
     width = mass_bb.shape[1]
     modes = fixed_modes.shape[2]
     slot_total = mass_ii.shape[0]
@@ -67,7 +76,7 @@
     spread_hot = jnp.broadcast_to(one_hot[:, None, :], (slot_total, sub_size, 2 * NBG))
     rows_in, hot_in = (
         lax.all_to_all(parts, "sub", split_axis=1, concat_axis=0, tiled=True),
-        lax.all_to_all(spread_hot, "sub", split_axis=1, concat_axis=0, tiled=True),
+        attach_column_on_mesh(spread_hot, "sub", row_dim=1, array_dim=0),
     )
     hot_flat = hot_in[:, 0, :]
     owned = jnp.einsum("rc,rab->cab", hot_flat, rows_in, precision=lax.Precision.HIGHEST)

time: 97.5 us -> 102 us (1.046)
  the two profiles are of different devices: /device:TPU:11 before, /device:TPU:0 now
where the time goes in v1:
time: 102 us; the launch traced here: 101 us
  local copies, waits for them, and re-layouts  32.6 us (32%)
  waiting for transfers between devices  27.3 us (27%)
  matrix products  23.9 us (23%)
  starting transfers between devices  15.7 us (15%)
  between operations  1.71 us (2%)
    dot_general x12, matrix products, contract(): lax.dot_general(left, right, (((0,), (0,)), ((), ())), preferred_element_...  18.7 us
    all_to_all x1, waiting for transfers between devices, per_device(): lax.all_to_all(parts, 'sub', split_axis=1, concat_axis=0, tiled=True)  18.7 us
    gather x9, local copies, waits for them, and re-layouts, per_device(): placed = reduced[inverse][:, inverse] * active  11 us
    all_to_all x1, starting transfers between devices, per_device(): lax.all_to_all(parts, 'sub', split_axis=1, concat_axis=0, tiled=True)  7.41 us
    all_to_all x1, starting transfers between devices, attach_column_on_mesh(): lax.all_to_all(jnp.stack(jnp.split(xx, lax.axis_size(link_axis), axis=row...  6.79 us
    unnamed x27, local copies, waits for them, and re-layouts  6.7 us
    all_to_all x1, waiting for transfers between devices, attach_column_on_mesh(): lax.all_to_all(jnp.stack(jnp.split(xx, lax.axis_size(link_axis), axis=row...  4.85 us
    dot_general x3, local copies, waits for them, and re-layouts, contract(): lax.dot_general(left, right, (((0,), (0,)), ((), ())), preferred_element_...  4.46 us
  transfers between devices with their start and end apart: 3, of which 3 were waited for; matrix products, arithmetic and copies ran while one was open for 8% of the time, Pallas kernels for 0%

profile of v1, /device:TPU:0, one launch (start us, length us, event | category | flops | bytes accessed | tf_op | source)
XLA Modules:
  0.0 101.5 jit_solution(6272469465471775551)
XLA Ops:
  0.6 0.0 copy-start
  0.6 2.4 %fusion.50 = f32[256,256]{1,0:T(8,128)} fusion(bf16[3,1024,256]{2,1,0:T(8,128)(2,1)} %param.12, bf16[3,1024,256]{2,1,0:T(8,128)(2,1)} %param.14), kind=kOutput, calls=%fused_computation.62 | convolution fusion | flops 134217728 | bytes 1310720 | tf_op jit(solution)/shard_map/dot_general | solution.py:15
  3.0 0.0 copy-done
  3.0 2.1 %fusion.38 = f32[256,256]{1,0:T(8,128)} fusion(bf16[3,1024,256]{2,1,0:T(8,128)(2,1)} %param.12, bf16[3,1024,256]{2,1,0:T(8,128)(2,1)S(1)} %copy-done), kind=kOutput, calls=%fused_computation.50 | convolution fusion | flops 134217728 | bytes 1310720 | tf_op jit(solution)/shard_map/dot_general | solution.py:15
  5.1 1.5 %fusion.44 = f32[256,256]{1,0:T(8,128)S(1)} fusion(bf16[3,1024,256]{2,1,0:T(8,128)(2,1)} %param.12, bf16[3,1024,256]{2,1,0:T(8,128)(2,1)S(1)} %copy-done), kind=kOutput, calls=%fused_computation.56 | convolution fusion | flops 134217728 | bytes 1310720 | tf_op jit(solution)/shard_map/dot_general | solution.py:15
  6.6 0.0 copy-start.3
  6.6 2.8 %fusion.9 = bf16[1024,256]{1,0:T(8,128)(2,1)S(1)} fusion(bf16[3,1024,1024]{2,1,0:T(8,128)(2,1)} %param.11, bf16[3,1024,256]{2,1,0:T(8,128)(2,1)S(1)} %copy-done), kind=kOutput, calls=%fused_computation.18 | convolution fusion | flops 537133056 | bytes 3145728 | tf_op jit(solution)/shard_map/dot_general | solution.py:21
  9.4 0.0 copy-done.10
  9.4 0.7 fusion.15
  10.1 0.0 copy-start.8
  10.1 0.7 fusion.12
  11.5 0.0 copy-done.8
  11.6 1.4 %scatter_custom_fusion = s32[256]{0:T(256)S(1)} fusion(s32[256]{0:T(256)S(1)} %bitcast.169, s32[256]{0:T(256)S(1)} %iota.22, s32[]{:T(128)} %constant.74.clone.1), kind=kCustom, calls=%fused_computation.114 | custom fusion | bytes 1028 | tf_op jit(solution)/shard_map/scatter | solution.py:63
  13.0 1.4 %scatter_custom_fusion.1 = s32[256]{0:T(256)S(1)} fusion(s32[256]{0:T(256)S(1)} %bitcast.168, s32[256]{0:T(256)S(1)} %iota.23, s32[]{:T(128)} %constant.74.clone.1), kind=kCustom, calls=%fused_computation.112 | custom fusion | bytes 1028 | tf_op jit(solution)/shard_map/scatter | solution.py:63
  14.4 1.4 %scatter_custom_fusion.2 = s32[256]{0:T(256)S(1)} fusion(s32[256]{0:T(256)S(1)} %bitcast.167, s32[256]{0:T(256)S(1)} %iota.24, s32[]{:T(128)} %constant.74.clone.1), kind=kCustom, calls=%fused_computation.110 | custom fusion | bytes 1028 | tf_op jit(solution)/shard_map/scatter | solution.py:63
  15.9 0.8 copy.53
  16.7 1.8 %copy.57 = f32[256,256]{0,1:T(8,128)} copy(f32[256,256]{1,0:T(8,128)} %fusion.38) | data formatting | bytes 524288 | tf_op jit(solution)/shard_map/dot_general | solution.py:15
  18.6 1.8 %copy.49 = f32[256,256]{0,1:T(8,128)} copy(f32[256,256]{1,0:T(8,128)} %fusion.50) | data formatting | bytes 524288 | tf_op jit(solution)/shard_map/dot_general | solution.py:15
  20.3 1.7 %fusion.89 = (bf16[1,256,256]{2,1,0:T(8,128)(2,1)}, bf16[1,256,256]{2,1,0:T(8,128)(2,1)}, bf16[1,256,256]{2,1,0:T(8,128)(2,1)S(1)}) fusion(bf16[3,256,256]{2,1,0:T(8,128)(2,1)} %param.13), kind=kLoop, calls=%fused_computation.116 | loop fusion | bytes 786432 | tf_op jit(solution)/shard_map/jit(dynamic_index_in_dim)/dynamic_slice | solution.py:47
  22.1 1.7 %copy.78 = bf16[1,256,256]{1,2,0:T(8,128)(2,1)} copy(bf16[1,256,256]{2,1,0:T(8,128)(2,1)} %get-tuple-element.8) | data formatting | bytes 262144
  23.7 1.7 %copy.77 = bf16[1,256,256]{1,2,0:T(8,128)(2,1)} copy(bf16[1,256,256]{2,1,0:T(8,128)(2,1)} %get-tuple-element.9) | data formatting | bytes 262144
  25.4 0.7 copy.76
  26.1 2.0 %fusion.26 = f32[256,256]{0,1:T(8,128)} fusion(f32[256,256]{0,1:T(8,128)} %copy.49, bf16[1024,256]{1,0:T(8,128)(2,1)S(1)} %fusion.9, bf16[3,1024,256]{2,1,0:T(8,128)(2,1)S(1)} %copy-done, f32[256,256]{1,0:T(8,128)S(1)} %copy-done.4, bf16[1,256,256]{1,2,0:T(8,128)(2,1)} %copy.76), kind=kOutput, calls=%fused_computation.32 | convolution fusion | flops 134479872 | bytes 1966080 | tf_op jit(solution)/shard_map/dot_general | solution.py:15
  28.2 1.1 %copy.51 = f32[256,256]{1,0:T(8,128)S(1)} copy(f32[256,256]{0,1:T(8,128)} %fusion.26) | data formatting | bytes 524288 | tf_op jit(solution)/shard_map/add | solution.py:25
  29.2 1.7 %gather_fusion = f32[256,256]{1,0:T(8,128)} fusion(f32[256,256]{1,0:T(8,128)S(1)} %copy.51, s32[1024]{0:T(1024)S(1)} %pad_clamp_fusion.2), kind=kCustom, calls=%fused_computation | custom fusion | bytes 525312 | tf_op jit(solution)/shard_map/gather | solution.py:65
  30.9 1.1 %copy.52 = f32[256,256]{0,1:T(8,128)S(1)} copy(f32[256,256]{1,0:T(8,128)} %gather_fusion) | data formatting | bytes 524288 | tf_op jit(solution)/shard_map/gather | solution.py:65
  32.0 1.7 %gather_fusion.1 = f32[256,256]{1,0:T(8,128)} fusion(f32[256,256]{0,1:T(8,128)S(1)} %copy.52, s32[1024]{0:T(1024)S(1)} %pad_clamp_fusion.2), kind=kCustom, calls=%fused_computation.1 | custom fusion | bytes 525312 | tf_op jit(solution)/shard_map/gather | solution.py:65
  33.7 0.0 copy-done.7
  33.7 2.1 %fusion.22 = f32[256,256]{0,1:T(8,128)} fusion(f32[256,256]{0,1:T(8,128)} %copy.57, bf16[1024,256]{1,0:T(8,128)(2,1)S(1)} %fusion.15, bf16[3,1024,256]{2,1,0:T(8,128)(2,1)S(1)} %copy-done, f32[256,256]{1,0:T(8,128)} %fusion.38, bf16[1,256,256]{1,2,0:T(8,128)(2,1)S(1)} %copy-done.7), kind=kOutput, calls=%fused_computation.28 | convolution fusion | flops 134479872 | bytes 1966080 | tf_op jit(solution)/shard_map/dot_general | solution.py:15
  35.8 1.1 %copy.59 = f32[256,256]{1,0:T(8,128)S(1)} copy(f32[256,256]{0,1:T(8,128)} %fusion.22) | data formatting | bytes 524288 | tf_op jit(solution)/shard_map/add | solution.py:25
  36.9 1.7 %gather_fusion.4 = f32[256,256]{1,0:T(8,128)} fusion(f32[256,256]{1,0:T(8,128)S(1)} %copy.59, s32[1024]{0:T(1024)S(1)} %pad_clamp_fusion), kind=kCustom, calls=%fused_computation.4 | custom fusion | bytes 525312 | tf_op jit(solution)/shard_map/gather | solution.py:65
  38.5 1.1 %copy.60 = f32[256,256]{0,1:T(8,128)S(1)} copy(f32[256,256]{1,0:T(8,128)} %gather_fusion.4) | data formatting | bytes 524288 | tf_op jit(solution)/shard_map/gather | solution.py:65
  39.6 1.7 %gather_fusion.5 = f32[256,256]{1,0:T(8,128)} fusion(f32[256,256]{0,1:T(8,128)S(1)} %copy.60, s32[1024]{0:T(1024)S(1)} %pad_clamp_fusion), kind=kCustom, calls=%fused_computation.5 | custom fusion | bytes 525312 | tf_op jit(solution)/shard_map/gather | solution.py:65
  41.3 1.4 %fusion.24 = f32[256,256]{0,1:T(8,128)S(1)} fusion(f32[256,256]{0,1:T(8,128)} %copy.53, bf16[1024,256]{1,0:T(8,128)(2,1)S(1)} %fusion.12, bf16[3,1024,256]{2,1,0:T(8,128)(2,1)S(1)} %copy-done, f32[256,256]{1,0:T(8,128)} %copy-done.3, bf16[1,256,256]{1,2,0:T(8,128)(2,1)S(1)} %copy-done.6), kind=kOutput, calls=%fused_computation.30 | convolution fusion | flops 134479872 | bytes 1966080 | tf_op jit(solution)/shard_map/dot_general | solution.py:15
  42.7 0.1 copy.55
  42.8 1.0 gather_fusion.2
  43.8 0.0 copy-start.1
  43.8 0.1 copy.56
  43.9 1.0 gather_fusion.3
  44.9 0.0 copy-start.2
  45.0 0.1 dynamic_update_slice.20
  45.1 0.8 copy-done.2
  45.9 1.3 %copy.61 = f32[3,256,256]{2,0,1:T(4,128)} copy(f32[3,256,256]{1,2,0:T(8,128)S(1)} %bitcast_dynamic-update-slice_fusion) | data formatting | bytes 1572864 | tf_op jit(solution)/shard_map/jit(dynamic_update_index_in_dim)/dynamic_update_slice | solution.py:66
  47.2 7.4 %all-to-all-start.1 = ((f32[3,256,256]{2,0,1:T(4,128)}), f32[3,256,256]{2,0,1:T(4,128)S(1)}, u32[]{:S(2)}, u32[]{:S(2)}) async-start(f32[3,256,256]{2,0,1:T(4,128)} %copy.61), calls=%async_computation.1 | async-start | bytes 2097152 | tf_op jit(solution)/shard_map/all_to_all | solution.py:78
  54.6 0.0 copy-start.9
  54.6 1.3 %convolution_bitcast_fusion.5 = f32[128,256]{0,1:T(8,128)S(1)} fusion(bf16[1024,256]{1,0:T(8,128)(2,1)S(1)} %fusion.9, bf16[3,1024,128]{2,1,0:T(8,128)(2,1)} %param.15), kind=kOutput, calls=%fused_computation.46 | convolution fusion | flops 67108864 | bytes 917504 | tf_op jit(solution)/shard_map/dot_general | solution.py:15
  55.9 1.5 %fusion.34 = f32[1,128,256]{1,2,0:T(8,128)S(1)} fusion(f32[128,256]{0,1:T(8,128)S(1)} %convolution_bitcast_fusion.5, bf16[3,1024,256]{2,1,0:T(8,128)(2,1)} %param.12, bf16[3,1024,128]{2,1,0:T(8,128)(2,1)} %param.15, f32[]{:T(128)S(6)} %convert_element_type.48), kind=kOutput, calls=%fused_computation.45 | convolution fusion | flops 67174400 | bytes 1048580 | tf_op jit(solution)/shard_map/dot_general | solution.py:15
  57.5 0.1 fusion.82
  57.5 1.3 %convolution_bitcast_fusion.4 = f32[128,256]{0,1:T(8,128)S(1)} fusion(bf16[1024,256]{1,0:T(8,128)(2,1)S(1)} %fusion.12, bf16[3,1024,128]{2,1,0:T(8,128)(2,1)} %param.15), kind=kOutput, calls=%fused_computation.42 | convolution fusion | flops 67108864 | bytes 917504 | tf_op jit(solution)/shard_map/dot_general | solution.py:15
  58.8 18.7 %all-to-all-done.1 = f32[3,256,256]{2,0,1:T(4,128)S(1)} async-done(((f32[3,256,256]{2,0,1:T(4,128)}), f32[3,256,256]{2,0,1:T(4,128)S(1)}, u32[]{:S(2)}, u32[]{:S(2)}) %all-to-all-start.1) | async-done | bytes 786464 | tf_op jit(solution)/shard_map/all_to_all | solution.py:78
  77.5 0.6 stack.2
  78.1 6.8 %all-to-all-start = ((f32[16,3,1,32]{3,2,1,0:T(1,128)}), f32[16,3,1,32]{3,2,1,0:T(1,128)S(1)}, u32[]{:S(2)}, u32[]{:S(2)}) async-start(f32[16,3,1,32]{3,2,1,0:T(1,128)} %stack.2), calls=%async_computation | async-start | bytes 49152 | tf_op jit(solution)/shard_map/all_to_all | solution.py:34
  84.9 1.5 %fusion.32 = f32[3,128,256]{1,2,0:T(8,128)S(1)} fusion(f32[3,128,256]{1,2,0:T(8,128)S(1)} %dynamic_update_slice.23, f32[128,256]{0,1:T(8,128)S(1)} %convolution_bitcast_fusion.4, bf16[3,1024,256]{2,1,0:T(8,128)(2,1)} %param.12, bf16[3,1024,128]{2,1,0:T(8,128)(2,1)} %param.15, f32[]{:T(128)S(6)} %convert_element_type.52), kind=kOutput, calls=%fused_computation.41 | convolution fusion | flops 67174400 | bytes 1048580 | tf_op jit(solution)/shard_map/dot_general | solution.py:15
  86.4 0.2 copy.62
  86.6 0.0 copy-start.5
  86.6 0.1 copy.63
  86.7 4.9 %all-to-all-done = f32[16,3,1,32]{3,2,1,0:T(1,128)S(1)} async-done(((f32[16,3,1,32]{3,2,1,0:T(1,128)}), f32[16,3,1,32]{3,2,1,0:T(1,128)S(1)}, u32[]{:S(2)}, u32[]{:S(2)}) %all-to-all-start) | async-done | bytes 6176 | tf_op jit(solution)/shard_map/all_to_all | solution.py:34
  91.5 1.0 %fusion.35 = f32[32,16,256]{2,0,1:T(8,128)S(1)} fusion(f32[48,32,1]{1,0,2:T(8,128)S(1)} %bitcast.166, f32[48,16,256]{2,1,0:T(8,128)S(1)} %bitcast.165), kind=kOutput, calls=%fused_computation.47 | convolution fusion | flops 75497472 | bytes 1316864 | tf_op jit(solution)/shard_map/rc,rab->cab/dot_general | solution.py:82
  92.6 1.5 %collective-permute-start = (f32[16,16,256]{2,0,1:T(8,128)S(1)}, f32[16,16,256]{2,0,1:T(8,128)S(1)}, u32[]{:S(2)}, u32[]{:S(2)}) collective-permute-start(f32[16,16,256]{2,0,1:T(8,128)S(1)} %slice.39), channel_id=1, source_target_pairs={{0,16},{16,0},{1,17},{17,1},{2,18},{18,2},{3,19},{19,3},{4,20},{20... | collective-permute-start | bytes 786440 | tf_op jit(solution)/shard_map/ppermute | solution.py:11
  94.1 0.3 convolution_bitcast_fusion.3
  94.5 1.4 %fusion.29 = f32[3,128,256]{1,2,0:T(8,128)S(1)} fusion(f32[3,128,256]{1,2,0:T(8,128)S(1)} %fusion.32, f32[128,256]{0,1:T(8,128)S(1)} %convolution_bitcast_fusion.3, bf16[3,1024,256]{2,1,0:T(8,128)(2,1)} %param.12, bf16[3,1024,128]{2,1,0:T(8,128)(2,1)S(1)} %copy-done.5, f32[]{:T(128)S(6)} %convert_element_type.56), kind=kOutput, calls=%fused_computation.36 | convolution fusion | flops 67174400 | bytes 1048580 | tf_op jit(solution)/shard_map/dot_general | solution.py:15
  95.9 0.9 copy.70
  96.8 3.8 %collective-permute-done = f32[16,16,256]{2,0,1:T(8,128)S(1)} collective-permute-done((f32[16,16,256]{2,0,1:T(8,128)S(1)}, f32[16,16,256]{2,0,1:T(8,128)S(1)}, u32[]{:S(2)}, u32[]{:S(2)}) %collective-permute-start) | collective-permute-done | bytes 262176 | tf_op jit(solution)/shard_map/ppermute | solution.py:11
  100.6 0.9 copy.69
  (26 shorter events, 0.2 us)
Async XLA Ops:
  0.6 2.4 %copy-start = (bf16[3,1024,256]{2,1,0:T(8,128)(2,1)S(1)}, bf16[3,1024,256]{2,1,0:T(8,128)(2,1)}, u32[]{:S(2)}) copy-start(bf16[3,1024,256]{2,1,0:T(8,128)(2,1)} %param.14) | copy-start | bytes 4718596
  5.1 4.3 %copy-start.10 = (bf16[3,1024,1024]{2,1,0:T(8,128)(2,1)S(1)}, bf16[3,1024,1024]{2,1,0:T(8,128)(2,1)}, u32[]{:S(2)}) copy-start(bf16[3,1024,1024]{2,1,0:T(8,128)(2,1)} %param.11) | copy-start | bytes 18874372
  6.6 9.3 %copy-start.3 = (f32[256,256]{1,0:T(8,128)}, f32[256,256]{1,0:T(8,128)S(1)}, u32[]{:S(2)}) copy-start(f32[256,256]{1,0:T(8,128)S(1)} %fusion.44) | copy-start | bytes 786436
  10.1 1.4 %copy-start.8 = (s32[3,256]{1,0:T(4,128)S(1)}, s32[3,256]{1,0:T(4,128)}, u32[]{:S(2)}) copy-start(s32[3,256]{1,0:T(4,128)} %param.10) | copy-start | bytes 9220
  16.7 9.4 %copy-start.4 = (f32[256,256]{1,0:T(8,128)S(1)}, f32[256,256]{1,0:T(8,128)}, u32[]{:S(2)}) copy-start(f32[256,256]{1,0:T(8,128)} %fusion.50) | copy-start | bytes 786436
  30.9 2.8 %copy-start.7 = (bf16[1,256,256]{1,2,0:T(8,128)(2,1)S(1)}, bf16[1,256,256]{1,2,0:T(8,128)(2,1)}, u32[]{:S(2)}) copy-start(bf16[1,256,256]{1,2,0:T(8,128)(2,1)} %copy.78) | copy-start | bytes 393220
  38.5 2.8 %copy-start.6 = (bf16[1,256,256]{1,2,0:T(8,128)(2,1)S(1)}, bf16[1,256,256]{1,2,0:T(8,128)(2,1)}, u32[]{:S(2)}) copy-start(bf16[1,256,256]{1,2,0:T(8,128)(2,1)} %copy.77) | copy-start | bytes 393220
  43.8 1.1 %copy-start.1 = (f32[256,256]{1,0:T(8,128)S(1)}, f32[256,256]{1,0:T(8,128)}, u32[]{:S(2)}) copy-start(f32[256,256]{1,0:T(8,128)} %gather_fusion.1) | copy-start | bytes 786436
  44.9 1.0 copy-start.2
  47.2 30.3 %all-to-all-start.1 = ((f32[3,256,256]{2,0,1:T(4,128)}), f32[3,256,256]{2,0,1:T(4,128)S(1)}, u32[]{:S(2)}, u32[]{:S(2)}) async-start(f32[3,256,256]{2,0,1:T(4,128)} %copy.61), calls=%async_computation.1 | async-start | bytes 2097152 | tf_op jit(solution)/shard_map/all_to_all | solution.py:78
  54.6 2.8 %copy-start.9 = (s32[3]{0:T(128)S(1)}, s32[3]{0:T(128)}, u32[]{:S(2)}) copy-start(s32[3]{0:T(128)} %param.9) | copy-start | bytes 40
  78.1 13.4 %all-to-all-start = ((f32[16,3,1,32]{3,2,1,0:T(1,128)}), f32[16,3,1,32]{3,2,1,0:T(1,128)S(1)}, u32[]{:S(2)}, u32[]{:S(2)}) async-start(f32[16,3,1,32]{3,2,1,0:T(1,128)} %stack.2), calls=%async_computation | async-start | bytes 49152 | tf_op jit(solution)/shard_map/all_to_all | solution.py:34
  86.6 7.5 %copy-start.5 = (bf16[3,1024,128]{2,1,0:T(8,128)(2,1)S(1)}, bf16[3,1024,128]{2,1,0:T(8,128)(2,1)}, u32[]{:S(2)}) copy-start(bf16[3,1024,128]{2,1,0:T(8,128)(2,1)} %param.15) | copy-start | bytes 2359300
  92.6 8.0 %collective-permute-start = (f32[16,16,256]{2,0,1:T(8,128)S(1)}, f32[16,16,256]{2,0,1:T(8,128)S(1)}, u32[]{:S(2)}, u32[]{:S(2)}) collective-permute-start(f32[16,16,256]{2,0,1:T(8,128)S(1)} %slice.39), channel_id=1, source_target_pairs={{0,16},{16,0},{1,17},{17,1},{2,18},{18,2},{3,19},{19,3},{4,20},{20... | collective-permute-start | bytes 786440 | tf_op jit(solution)/shard_map/ppermute | solution.py:11
